TPU v7x, 32 devices: a whole 2x2x4 slice. The times are simulated.
32 devices in a mesh: tile: 16 (over z, x, core), mem: 2 (over y).
Axes of the slice: x: 2, y: 2, z: 4, core: 2. Of those that a mesh axis runs over, the one named last changes fastest.
Arguments:
- anomalies: bfloat16 [80, 137, 2048], P('mem', None, 'tile'), may hold values from -6 to 6
- analysis_weights: bfloat16 [16, 80, 80], P('tile'), may hold values from -0.6 to 1.7
- background_mean: bfloat16 [137, 2048], P(None, 'tile'), may hold values from -6 to 6
- background: bfloat16 [80, 137, 2048], P('mem', None, 'tile'), may hold values from -6 to 6
- jacobian_table: bfloat16 [8461, 137], replicated, may hold values from -0.5 to 0.5
- channel_list: int32 [96], replicated, may hold values from 0 to 8460
- send_slots: int32 [16, 16, 32], P('tile'), may hold values from -1 to 127, as said below
- footprint: int32 [8192, 4], P('tile'), may hold values from 0 to 511, as said below
- footprint_weight: bfloat16 [8192, 4], P('tile'), may hold values from 0.25 to 1
- channel_bias: float32 [96], replicated, may hold values from -4 to 4
Outputs:
- analysis_members: bfloat16 [80, 137, 2048], P('mem', None, 'tile')
- radiance_prior: float32 [96, 80, 8192], P(None, 'mem', 'tile')
Inputs may be any that keep to these rules, and one draw needn't show every extreme that they name: `send_slots`: entry [s, d, i] is a column within owner s's block of 128 columns that owner s sends to tile d in slot i, or -1 for an empty slot; the filled slots of a pair come first, each pair fills 1 to 32 slots, and in every draw one tile receives 32 filled slots from every owner. `footprint`: entry [o, j] is a slot of the buffer of observation o's tile, which holds 32 slots from each owner in owner order; every entry names a filled slot, the 4 entries of a row differ, and every filled slot is named by some row of that tile.
All inputs are finite; a program needn't handle non-finite values.
Results may differ from a plain program's by a relative error of at most 0.0021.
Values may be sent and summed in bfloat16 or wider, within the bound.
A program may use at most 128 MiB of HBM per device.

v0:
```python
import jax
import jax.numpy as jnp
from jax import lax
from jax.sharding import PartitionSpec as P

GROUP = 128
FOOT = 4


def shards(
    anomalies,
    analysis_weights,
    background_mean,
    background,
    jacobian_table,
    channel_list,
    send_slots,
    footprint,
    footprint_weight,
    channel_bias,
):
    mem_dev = anomalies.shape[0]
    levels = anomalies.shape[1]
    columns_dev = anomalies.shape[2]
    groups = columns_dev // GROUP
    mean_float = background_mean.astype(jnp.float32)
    member_start = lax.axis_index("mem") * mem_dev
    member_piece = lax.all_gather(anomalies, "mem", axis=0, tiled=True)
    piece_rows = member_piece.shape[0]
    weight_rows = analysis_weights
    weight_rows = lax.dynamic_slice_in_dim(weight_rows, member_start, mem_dev, 2)
    reshaped = member_piece.reshape(piece_rows, levels, groups, GROUP)
    mixture = jnp.einsum(
        "klgc,gkm->mlgc", reshaped, weight_rows, preferred_element_type=jnp.float32
    )
    analysis_members = (mixture.reshape(mem_dev, levels, columns_dev) + mean_float[None]).astype(
        jnp.bfloat16
    )
    selected = jnp.take(jacobian_table, channel_list, axis=0)
    slot_cols = jnp.maximum(send_slots[0], 0).reshape(-1)
    owned = jnp.einsum(
        "cl,klx->ckx", selected, background, preferred_element_type=jnp.float32
    ).astype(jnp.bfloat16)
    packed = jnp.take(owned, slot_cols, axis=2)
    received = lax.all_to_all(packed, "tile", split_axis=2, concat_axis=2, tiled=True)
    channels = received.shape[0]
    obs_count = footprint.shape[0]
    picked = jnp.take(received, footprint.reshape(-1), axis=2).reshape(
        channels, mem_dev, obs_count, FOOT
    )
    weighted = picked.astype(jnp.float32) * footprint_weight.astype(jnp.float32)[None, None]
    prior_out = jnp.sum(weighted, axis=3) + channel_bias[:, None, None]
    return (analysis_members, prior_out)


def solution(mesh):
    placed = (
        P("mem", None, "tile"),
        P("tile", None, None),
        P(None, "tile"),
        P("mem", None, "tile"),
        P(),
        P(),
        P("tile", None, None),
        P("tile", None),
        P("tile", None),
        P(),
    )
    return jax.shard_map(
        shards,
        mesh=mesh,
        in_specs=placed,
        out_specs=(P("mem", None, "tile"), P(None, "mem", "tile")),
        check_vma=False,
    )
```

profile of v0, /device:TPU:11, one launch (start us, length us, event | category | flops | bytes accessed | tf_op | source)
XLA Modules:
  0.0 223.6 jit_solution(4446422956958889436)
XLA Ops:
  7.2 0.0 copy-start
  7.2 0.8 compare_and_fusion.1
  8.0 0.7 compare_select_fusion.2
  8.6 0.7 broadcast_compare_fusion
  9.3 0.7 broadcast_maximum_fusion
  10.0 0.1 le.39
  10.1 0.1 reshape.96
  10.2 5.6 %copy.28 = bf16[8461,137]{1,0:T(8,128)(2,1)} copy(bf16[8461,137]{0,1:T(8,128)(2,1)} %param.14) | data formatting | bytes 4636628 | tf_op args[4]
  15.8 3.5 %gather_fusion = bf16[96,137]{1,0:T(8,128)(2,1)S(1)} fusion(bf16[8461,137]{1,0:T(8,128)(2,1)} %copy.28, s32[1024]{0:T(1024)S(1)} %pad_clamp_fusion.1), kind=kCustom, calls=%fused_computation | custom fusion | bytes 52992 | tf_op jit(solution)/shard_map/jit(_take)/gather | solution.py:39
  19.2 0.0 copy-done
  19.3 0.5 fusion.2
  19.7 1.4 copy.31
  21.2 4.0 %gather_fusion.1 = bf16[512,96,40]{1,2,0:T(8,128)(2,1)} fusion(bf16[96,40,128]{0,1,2:T(8,128)(2,1)S(1)} %copy.31, s32[1024]{0:T(1024)S(1)} %pad_clamp_fusion), kind=kCustom, calls=%fused_computation.1 | custom fusion | bytes 7866368 | tf_op jit(solution)/shard_map/jit(_take)/gather | solution.py:44
  25.1 6.6 %select_bitcast_fusion = bf16[96,40,512]{0,1,2:T(8,128)(2,1)} fusion(bf16[512,96,40]{1,2,0:T(8,128)(2,1)} %gather_fusion.1, pred[512]{0:T(512)(128)(4,1)S(1)} %le.39), kind=kLoop, calls=%fused_computation.4 | loop fusion | flops 1966080 | bytes 7864832 | tf_op jit(solution)/shard_map/jit(_take)/select_n | solution.py:44
  31.7 6.7 %all-to-all-start = ((bf16[96,40,512]{0,1,2:T(8,128)(2,1)}), bf16[96,40,512]{0,1,2:T(8,128)(2,1)}, u32[]{:S(2)}, u32[]{:S(2)}) async-start(bf16[96,40,512]{0,1,2:T(8,128)(2,1)} %select_bitcast_fusion), calls=%async_computation | async-start | bytes 10485760 | tf_op jit(solution)/shard_map/all_to_all | solution.py:45
  38.4 0.0 all-gather.2.cloned.1.call-start
  38.5 0.7 all-gather.2.cloned.1.call-update
  39.1 0.0 copy-done.3
  39.2 0.1 copy.32
  39.3 0.2 copy.27
  39.5 0.0 copy-done.2
  39.5 0.0 copy-done.5
  39.6 0.1 copy.33
  39.7 0.2 reshape.85
  39.9 42.4 %all-gather.2.cloned.1.call-done = bf16[80,137,128]{2,0,1:T(8,128)(2,1)} async-done(((bf16[40,137,128]{2,0,1:T(8,128)(2,1)}), bf16[80,137,128]{2,0,1:T(8,128)(2,1)}) %all-gather.2.cloned.1.call-update) | async-done | bytes 2805776 | tf_op jit(solution)/shard_map/all_gather | solution.py:28
  82.3 0.0 copy-done.4
  82.3 3.5 %add_convert_fusion = bf16[40,137,128]{2,0,1:T(8,128)(2,1)} fusion(bf16[80,137,128]{2,0,1:T(8,128)(2,1)} %all-gather.2.cloned.1.call-done, f32[137,128]{1,0:T(8,128)S(1)} %convert_element_type.15, bf16[1,80,80]{2,1,0:T(8,128)(2,1)S(1)} %copy-done.4, s32[]{:T(128)S(6)} %select_n.44), kind=kOutput, calls=%fused_computation.6 | convolution fusion | flops 113633280 | bytes 4291588 | tf_op jit(solution)/shard_map/klgc,gkm->mlgc/dot_general | solution.py:33
  85.9 67.5 %all-to-all-done = bf16[96,40,512]{0,1,2:T(8,128)(2,1)} async-done(((bf16[96,40,512]{0,1,2:T(8,128)(2,1)}), bf16[96,40,512]{0,1,2:T(8,128)(2,1)}, u32[]{:S(2)}, u32[]{:S(2)}) %all-to-all-start) | async-done | bytes 3932192 | tf_op jit(solution)/shard_map/all_to_all | solution.py:45
  153.3 24.0 %gather_fusion.2 = bf16[2048,96,40]{1,2,0:T(8,128)(2,1)} fusion(bf16[96,40,512]{0,1,2:T(8,128)(2,1)} %all-to-all-done, s32[2048]{0:T(1024)S(1)} %broadcast_clamp_fusion), kind=kCustom, calls=%fused_computation.2 | custom fusion | bytes 31465472 | tf_op jit(solution)/shard_map/jit(_take)/gather | solution.py:48
  177.4 19.8 %multiply_reduce_fusion = f32[96,40,512]{0,1,2:T(8,128)} fusion(f32[512,4]{1,0:T(8,128)S(1)} %copy.33, pred[512,4]{1,0:T(8,128)(4,1)S(1)} %copy.27, bf16[2048,96,40]{1,2,0:T(8,128)(2,1)} %gather_fusion.2), kind=kLoop, calls=%fused_computation.3 | loop fusion | flops 29491200 | bytes 23603200 | tf_op jit(solution)/shard_map/reduce_sum | solution.py:52
  197.2 8.7 %broadcast_add_fusion = f32[96,40,512]{0,1,2:T(8,128)} fusion(f32[96,40,512]{0,1,2:T(8,128)} %multiply_reduce_fusion, f32[96]{0:T(128)S(1)} %copy-done.6), kind=kLoop, calls=%fused_computation.5 | loop fusion | flops 1966080 | bytes 15729024 | tf_op jit(solution)/shard_map/add | solution.py:52
  205.9 10.8 %copy.34 = f32[96,40,512]{2,1,0:T(8,128)} copy(f32[96,40,512]{0,1,2:T(8,128)} %broadcast_add_fusion) | data formatting | bytes 15728640
  (14 shorter events, 0.1 us)
Async XLA Ops:
  7.2 12.1 %copy-start = (bf16[40,137,128]{2,0,1:T(8,128)(2,1)S(1)}, bf16[40,137,128]{2,0,1:T(8,128)(2,1)}, u32[]{:S(2)}) copy-start(bf16[40,137,128]{2,0,1:T(8,128)(2,1)} %param.13) | copy-start | bytes 4208644
  31.7 7.4 %copy-start.3 = (s32[512,4]{0,1:T(4,128)S(1)}, s32[512,4]{0,1:T(4,128)}, u32[]{:S(2)}) copy-start(s32[512,4]{0,1:T(4,128)} %param.17) | copy-start | bytes 24580
  31.7 7.8 %copy-start.2 = (bf16[137,128]{1,0:T(8,128)(2,1)S(1)}, bf16[137,128]{1,0:T(8,128)(2,1)}, u32[]{:S(2)}) copy-start(bf16[137,128]{1,0:T(8,128)(2,1)} %param.12) | copy-start | bytes 105220
  31.7 7.8 %copy-start.5 = (bf16[512,4]{0,1:T(4,128)(2,1)S(1)}, bf16[512,4]{0,1:T(4,128)(2,1)}, u32[]{:S(2)}) copy-start(bf16[512,4]{0,1:T(4,128)(2,1)} %param.18) | copy-start | bytes 12292
  31.7 50.6 %copy-start.4 = (bf16[1,80,80]{2,1,0:T(8,128)(2,1)S(1)}, bf16[1,80,80]{2,1,0:T(8,128)(2,1)}, u32[]{:S(2)}) copy-start(bf16[1,80,80]{2,1,0:T(8,128)(2,1)} %param.11) | copy-start | bytes 38404
  31.7 121.6 %all-to-all-start = ((bf16[96,40,512]{0,1,2:T(8,128)(2,1)}), bf16[96,40,512]{0,1,2:T(8,128)(2,1)}, u32[]{:S(2)}, u32[]{:S(2)}) async-start(bf16[96,40,512]{0,1,2:T(8,128)(2,1)} %select_bitcast_fusion), calls=%async_computation | async-start | bytes 10485760 | tf_op jit(solution)/shard_map/all_to_all | solution.py:45
  38.4 43.9 %all-gather.2.cloned.1.call-start = ((), (), s32[]{:S(2)}) async-start(), calls=%async_computation.1 | async-start | bytes 4208640 | tf_op jit(solution)/shard_map/all_gather | solution.py:28
  177.4 19.9 %copy-start.6 = (f32[96]{0:T(128)S(1)}, f32[96]{0:T(128)}, u32[]{:S(2)}) copy-start(f32[96]{0:T(128)} %param.19) | copy-start | bytes 1156
  197.2 19.6 %copy-start.1 = (bf16[40,137,128]{2,0,1:T(8,128)(2,1)S(1)}, bf16[40,137,128]{2,0,1:T(8,128)(2,1)}, u32[]{:S(2)}) copy-start(bf16[40,137,128]{2,0,1:T(8,128)(2,1)} %param.13) | copy-start | bytes 4208644
Sparse Core Ops, SparseCore 0:
  40.8 41.5 all-gather.1
where the time goes:
time: 224 us
  waiting for transfers between devices  111 us (50%)
  local copies, waits for them, and re-layouts  50.1 us (22%)
  other arithmetic  38 us (17%)
  between operations  14.2 us (6%)
  starting transfers between devices  6.7 us (3%)
  matrix products  4.01 us (2%)
    all_to_all x1, waiting for transfers between devices, shards(): lax.all_to_all(packed, 'tile', split_axis=2, concat_axis=2, tiled=True)  67.5 us
    all_gather x1, waiting for transfers between devices, shards(): member_piece = lax.all_gather(anomalies, 'mem', axis=0, tiled=True)  42.4 us
    gather x1, local copies, waits for them, and re-layouts, shards(): jnp.take(received, footprint.reshape(-1), axis=2)  24 us
    reduce_sum x1, other arithmetic, shards(): prior_out = jnp.sum(weighted, axis=3) + channel_bias[:, None, None]  19.8 us
    unnamed x17, local copies, waits for them, and re-layouts  16.6 us
    add x1, other arithmetic, shards(): prior_out = jnp.sum(weighted, axis=3) + channel_bias[:, None, None]  8.72 us
    all_to_all x1, starting transfers between devices, shards(): lax.all_to_all(packed, 'tile', split_axis=2, concat_axis=2, tiled=True)  6.67 us
    select_n x1, other arithmetic, shards(): packed = jnp.take(owned, slot_cols, axis=2)  6.6 us
  transfers between devices with their start and end apart: 2, of which 2 were waited for; matrix products, arithmetic and copies ran while one was open for 2% of the time, Pallas kernels for 0%

commit v1 on v0

v1 whole, which is shorter than its diff:
```python
import functools

import jax
import jax.numpy as jnp
from jax import lax
from jax.experimental import pallas as pl
from jax.experimental.pallas import tpu as pltpu
from jax.sharding import PartitionSpec as P

LANES = 128
MESH = pl.DeviceIdType.MESH


def exchange_kernel(
    n,
    nm,
    owned_ref,
    target_ref,
    anom_ref,
    weight_ref,
    mean_ref,
    foot_ref,
    fweight_ref,
    recv_ref,
    analysis_ref,
    spread_ref,
    send_buf,
    pieces,
    mixed,
    spread,
    a_send,
    a_recv,
    m_send,
    m_recv,
    local_sem,
):
    tile = lax.axis_index("tile")
    mem = lax.axis_index("mem")
    groups, rows, cols = owned_ref.shape
    chips = n // 2
    slots = spread_ref.shape[0] // n
    obs = spread_ref.shape[1]
    levels = anom_ref.shape[0]

    barrier = pltpu.get_barrier_semaphore()

    def greet(k, carry):
        pl.semaphore_signal(
            barrier, inc=1, device_id=(lax.rem(tile + k, n), mem), device_id_type=MESH
        )
        return carry

    lax.fori_loop(1, n, greet, 0)
    for k in range(1, nm):
        pl.semaphore_signal(
            barrier, inc=1, device_id=(tile, lax.rem(mem + k, nm)), device_id_type=MESH
        )
    own_piece = pltpu.make_async_copy(anom_ref, pieces.at[mem], local_sem.at[0])
    own_piece.start()
    pl.semaphore_wait(barrier, n - 1 + nm - 1)

    def member_copy(k):
        peer = lax.rem(mem + k, nm)
        return pltpu.make_async_remote_copy(
            src_ref=anom_ref,
            dst_ref=pieces.at[mem],
            send_sem=m_send.at[k],
            recv_sem=m_recv.at[k],
            device_id=(tile, peer),
            device_id_type=MESH,
        )

    for k in range(1, nm):
        member_copy(k).start()

    def tile_copy(dest):
        return pltpu.make_async_remote_copy(
            src_ref=send_buf.at[dest],
            dst_ref=recv_ref.at[tile],
            send_sem=a_send.at[dest],
            recv_sem=a_recv.at[tile],
            device_id=(dest, mem),
            device_id_type=MESH,
        )

    def arrival(source):
        return pltpu.make_async_remote_copy(
            src_ref=send_buf.at[source],
            dst_ref=recv_ref.at[source],
            send_sem=a_send.at[source],
            recv_sem=a_recv.at[source],
            device_id=(source, mem),
            device_id_type=MESH,
        )

    my_chip = tile // 2

    def chip_at(p):
        step = ((p + 1) // 2) * (1 - 2 * lax.rem(p + 1, 2))
        return lax.rem(my_chip + step + chips, chips)

    wide = jnp.concatenate([owned_ref[g] for g in range(groups)], axis=1)
    row_id = lax.broadcasted_iota(jnp.int32, (groups * cols, 2 * LANES), 0)

    def pack(chip):
        first = chip * 2
        want = jnp.concatenate([target_ref[first], target_ref[first + 1]], axis=1)
        pick = jnp.where(row_id == want, 1.0, 0.0).astype(jnp.bfloat16)
        out = jnp.dot(wide, pick, preferred_element_type=jnp.float32).astype(jnp.bfloat16)
        send_buf[first] = out[:, :LANES]
        send_buf[first + 1] = out[:, LANES:]

    def send(chip):
        for core in range(2):
            tile_copy(chip * 2 + core).start()

    pack(chip_at(1))

    def step(p, carry):
        pack(chip_at(p))
        send(chip_at(p - 1))
        return carry

    lax.fori_loop(2, chips, step, 0)
    pack(my_chip)
    send(chip_at(chips - 1))
    other = my_chip * 2 + 1 - lax.rem(tile, 2)

    fweight = fweight_ref[...].astype(jnp.float32)

    def spread_rows(s, carry):
        ids = lax.broadcasted_iota(jnp.int32, (slots, obs), 0) + s * slots
        total = jnp.zeros((slots, obs), jnp.float32)
        for j in range(foot_ref.shape[0]):
            total = total + jnp.where(
                ids == foot_ref[j : j + 1, :], fweight[j : j + 1, :], 0.0
            )
        spread[pl.ds(pl.multiple_of(s * slots, slots), slots), :] = total.astype(jnp.bfloat16)
        return carry

    lax.fori_loop(0, n, spread_rows, 0)
    tile_copy(other).start()
    own_chunk = pltpu.make_async_copy(send_buf.at[tile], recv_ref.at[tile], local_sem.at[1])
    own_chunk.start()

    own_piece.wait()
    spread_out = pltpu.make_async_copy(spread, spread_ref, local_sem.at[2])
    spread_out.start()
    for k in range(1, nm):
        member_copy(k).wait()

    def mix(l, carry):
        total = jnp.broadcast_to(
            mean_ref[l].astype(jnp.float32), (weight_ref.shape[1], cols)
        )
        mixture = jnp.zeros_like(total)
        for p in range(nm):
            mixture = mixture + jnp.dot(
                weight_ref[p], pieces[p, l], preferred_element_type=jnp.float32
            )
        mixed[l] = (total + mixture).astype(jnp.bfloat16)
        return carry

    lax.fori_loop(0, levels, mix, 0)

    def drain(k, carry):
        source = lax.rem(tile + k, n)
        arrival(source).wait()
        return carry

    lax.fori_loop(1, n // 2, drain, 0)
    analysis_out = pltpu.make_async_copy(mixed, analysis_ref, local_sem.at[3])
    analysis_out.start()
    lax.fori_loop(n // 2, n, drain, 0)
    own_chunk.wait()
    spread_out.wait()
    analysis_out.wait()


def combine_kernel(n, groups, per_step, bias_ref, recv_ref, spread_ref, out_ref):
    step = pl.program_id(0)
    slots = spread_ref.shape[0] // n
    per_group = out_ref.shape[1] * pl.num_programs(0)
    members = out_ref.shape[2]
    blocks = [recv_ref[s] for s in range(n)]
    for g in range(groups):
        lanes = slice(g * slots, (g + 1) * slots)
        stacked = jnp.concatenate([block[:, lanes] for block in blocks], axis=1)
        prior = jnp.dot(stacked, spread_ref[...], preferred_element_type=jnp.float32)
        for c in range(per_step):
            bias = bias_ref[g * per_group + step * per_step + c]
            out_ref[g, c] = prior[c * members : (c + 1) * members, :] + bias


def shards(
    n,
    nm,
    anomalies,
    analysis_weights,
    background_mean,
    background,
    jacobian_table,
    channel_list,
    send_slots,
    footprint,
    footprint_weight,
    channel_bias,
):
    mem_dev, levels, cols = anomalies.shape
    channels = channel_list.shape[0]
    slots = send_slots.shape[2]
    obs = footprint.shape[0]
    groups = LANES // slots
    rows = channels * mem_dev // groups
    mem = lax.axis_index("mem")

    chosen = (
        jnp.arange(jacobian_table.shape[0], dtype=jnp.int32)[:, None] == channel_list[None, :]
    ).astype(jnp.bfloat16)
    selected = jnp.einsum(
        "sl,sc->cl", jacobian_table, chosen, preferred_element_type=jnp.float32
    ).astype(jnp.bfloat16)
    owned = jnp.einsum(
        "cl,klx->ckx", selected, background, preferred_element_type=jnp.float32
    ).astype(jnp.bfloat16)
    owned = owned.reshape(groups, rows, cols)
    lane_rows = jnp.maximum(send_slots[0], 0)[:, None, :] + (
        jnp.arange(groups, dtype=jnp.int32) * cols
    )[None, :, None]
    target = lane_rows.reshape(n, 1, LANES)
    weights = lax.dynamic_slice_in_dim(analysis_weights[0], mem * mem_dev, mem_dev, 1)
    weights = jnp.transpose(weights.reshape(nm, mem_dev, mem_dev), (0, 2, 1))
    vmem = pl.BlockSpec(memory_space=pltpu.VMEM)
    hbm = pl.BlockSpec(memory_space=pl.ANY)
    received, analysis, spread = pl.pallas_call(
        functools.partial(exchange_kernel, n, nm),
        out_shape=(
            jax.ShapeDtypeStruct((n, rows, LANES), jnp.bfloat16),
            jax.ShapeDtypeStruct((levels, mem_dev, cols), jnp.bfloat16),
            jax.ShapeDtypeStruct((n * slots, obs), jnp.bfloat16),
        ),
        in_specs=[vmem, vmem, hbm, vmem, vmem, vmem, vmem],
        out_specs=(hbm, hbm, hbm),
        scratch_shapes=[
            pltpu.VMEM((n, rows, LANES), jnp.bfloat16),
            pltpu.VMEM((nm, levels, mem_dev, cols), jnp.bfloat16),
            pltpu.VMEM((levels, mem_dev, cols), jnp.bfloat16),
            pltpu.VMEM((n * slots, obs), jnp.bfloat16),
            pltpu.SemaphoreType.DMA((n,)),
            pltpu.SemaphoreType.DMA((n,)),
            pltpu.SemaphoreType.DMA((nm,)),
            pltpu.SemaphoreType.DMA((nm,)),
            pltpu.SemaphoreType.DMA((4,)),
        ],
        compiler_params=pltpu.CompilerParams(
            collective_id=0, has_side_effects=True, vmem_limit_bytes=48 * 1024 * 1024
        ),
        name="exchange",
    )(
        owned,
        target,
        jnp.transpose(anomalies, (1, 0, 2)),
        weights,
        background_mean[:, None, :],
        jnp.transpose(footprint),
        jnp.transpose(footprint_weight),
    )
    analysis_members = jnp.transpose(analysis, (1, 0, 2))

    per_group = channels // groups
    per_step = next(c for c in (4, 8, per_group) if c * mem_dev % 16 == 0)
    prior = pl.pallas_call(
        functools.partial(combine_kernel, n, groups, per_step),
        out_shape=jax.ShapeDtypeStruct((groups, per_group, mem_dev, obs), jnp.float32),
        grid=(per_group // per_step,),
        in_specs=[
            pl.BlockSpec(memory_space=pltpu.SMEM),
            pl.BlockSpec((n, per_step * mem_dev, LANES), lambda i: (0, i, 0)),
            pl.BlockSpec((n * slots, obs), lambda i: (0, 0)),
        ],
        out_specs=pl.BlockSpec((groups, per_step, mem_dev, obs), lambda i: (0, i, 0, 0)),
        compiler_params=pltpu.CompilerParams(vmem_limit_bytes=48 * 1024 * 1024),
        name="combine",
    )(channel_bias, received, spread)
    return analysis_members, prior.reshape(channels, mem_dev, obs)


def solution(mesh):
    placed = (
        P("mem", None, "tile"),
        P("tile", None, None),
        P(None, "tile"),
        P("mem", None, "tile"),
        P(),
        P(),
        P("tile", None, None),
        P("tile", None),
        P("tile", None),
        P(),
    )
    return jax.shard_map(
        functools.partial(shards, mesh.shape["tile"], mesh.shape["mem"]),
        mesh=mesh,
        in_specs=placed,
        out_specs=(P("mem", None, "tile"), P(None, "mem", "tile")),
        check_vma=False,
    )
```

time: 224 us -> 112 us (0.50)
  the two profiles are of different devices: /device:TPU:11 before, /device:TPU:1 now
where the time goes in v1:
time: 112 us
  Pallas kernels  100 us (89%)
  local copies, waits for them, and re-layouts  6.5 us (6%)
  matrix products  3.21 us (3%)
    pallas_call x1, Pallas kernels, shards(): pl.pallas_call(functools.partial(exchange_kernel, n, nm), out_shape=(jax....  93.3 us
    pallas_call x1, Pallas kernels, shards(): pl.pallas_call(functools.partial(combine_kernel, n, groups, per_step), ou...  6.95 us
    unnamed x13, local copies, waits for them, and re-layouts  4.14 us
    dot_general x1, matrix products, shards(): jnp.einsum('cl,klx->ckx', selected, background, preferred_element_type=jn...  3.21 us

profile of v1, /device:TPU:1, one launch (start us, length us, event | category | flops | bytes accessed | tf_op | source)
XLA Modules:
  0.0 111.6 jit_solution(4058948743663769425)
XLA Ops:
  0.6 0.0 copy-start
  0.7 0.1 add.31
  0.7 0.1 add.32
  0.8 0.8 maximum_bitcast_fusion
  1.7 0.8 constant_dynamic-slice_fusion
  2.5 0.1 copy.17
  2.6 0.1 add.30
  2.7 0.8 copy.18.mean_ref
  3.5 0.0 copy-done
  3.5 3.2 %fusion.4 = bf16[96,40,128]{2,0,1:T(8,128)(2,1)S(1)} fusion(bf16[40,137,128]{2,0,1:T(8,128)(2,1)} %param.13, bf16[8461,137]{0,1:T(8,128)(2,1)S(1)} %copy-done, s32[96]{0:T(128)} %param.15), kind=kOutput, calls=%fused_computation.5 | convolution fusion | flops 358551552 | bytes 4704618 | tf_op jit(solution)/shard_map/cl,klx->ckx/dot_general | solution.py:223
  6.7 0.0 copy-start.2
  6.7 0.0 copy-start.3
  6.8 0.0 copy-start.4
  6.8 0.0 copy-start.5
  6.8 0.4 copy.15
  7.2 0.9 copy-done.2
  8.1 0.0 copy-done.3
  8.1 0.0 copy-done.4
  8.1 93.3 %exchange.1 = (bf16[16,960,128]{2,1,0:T(8,128)(2,1)}, bf16[137,40,128]{2,1,0:T(8,128)(2,1)S(1)}, bf16[512,512]{1,0:T(8,128)(2,1)S(1)}) custom-call(bf16[4,960,128]{2,1,0:T(8,128)(2,1)S(1)} %bitcast.16, s32[16,1,128]{2,1,0:T(1,128)S(1)} %broadcast_add_fusion.target_ref, bf16[137,40,128]{2,1,0:T(8,128)(2,1)S(1)} %bitcast.17, bf16[2,40,40]{2,1,0:T(8,128)(2,1)S(1)} %bitcast.19, ...), custom_call_target="tpu_custom_call" | custom-call | tf_op jit(solution)/shard_map/exchange/pallas_call | solution.py:235
  101.4 0.0 copy-done.5
  101.4 0.0 copy-start.1
  101.5 2.1 %copy-done.1 = bf16[16,960,128]{2,1,0:T(8,128)(2,1)S(1)} copy-done((bf16[16,960,128]{2,1,0:T(8,128)(2,1)S(1)}, bf16[16,960,128]{2,1,0:T(8,128)(2,1)}, u32[]{:S(2)}) %copy-start.1) | copy-done | bytes 3932184
  103.6 7.0 %combine.1 = f32[4,24,40,512]{3,2,1,0:T(8,128)} custom-call(f32[96]{0:T(128)S(1)} %copy-done.5, bf16[16,960,128]{2,1,0:T(8,128)(2,1)S(1)} %copy-done.1, bf16[512,512]{1,0:T(8,128)(2,1)S(1)} %get-tuple-element.7.spread_ref), custom_call_target="tpu_custom_call" | custom-call | tf_op jit(solution)/shard_map/combine/pallas_call | solution.py:272
  110.5 1.1 copy.26
  (3 shorter events, 0.0 us)
Async XLA Ops:
  0.6 2.9 %copy-start = (bf16[8461,137]{0,1:T(8,128)(2,1)S(1)}, bf16[8461,137]{0,1:T(8,128)(2,1)}, u32[]{:S(2)}) copy-start(bf16[8461,137]{0,1:T(8,128)(2,1)} %param.14) | copy-start | bytes 6954946
  6.7 1.4 %copy-start.2 = (bf16[40,137,128]{2,0,1:T(8,128)(2,1)S(1)}, bf16[40,137,128]{2,0,1:T(8,128)(2,1)}, u32[]{:S(2)}) copy-start(bf16[40,137,128]{2,0,1:T(8,128)(2,1)} %param.10) | copy-start | bytes 4208644
  6.7 1.3 %copy-start.3 = (s32[512,4]{0,1:T(4,128)S(1)}, s32[512,4]{0,1:T(4,128)}, u32[]{:S(2)}) copy-start(s32[512,4]{0,1:T(4,128)} %param.17) | copy-start | bytes 24580
  6.8 1.3 %copy-start.4 = (bf16[512,4]{0,1:T(4,128)(2,1)S(1)}, bf16[512,4]{0,1:T(4,128)(2,1)}, u32[]{:S(2)}) copy-start(bf16[512,4]{0,1:T(4,128)(2,1)} %param.18) | copy-start | bytes 12292
  6.8 94.7 %copy-start.5 = (f32[96]{0:T(128)S(1)}, f32[96]{0:T(128)}, u32[]{:S(2)}) copy-start(f32[96]{0:T(128)} %bias_ref.1) | copy-start | bytes 1156
  101.4 2.1 %copy-start.1 = (bf16[16,960,128]{2,1,0:T(8,128)(2,1)S(1)}, bf16[16,960,128]{2,1,0:T(8,128)(2,1)}, u32[]{:S(2)}) copy-start(bf16[16,960,128]{2,1,0:T(8,128)(2,1)} %get-tuple-element.6.recv_ref) | copy-start | bytes 11796484

commit v2 on v1

--- a/solution.py
+++ b/solution.py
@@ -25,6 +25,9 @@
     analysis_ref,
     spread_ref,
     send_buf,
+    relay_buf,
+    relay_block,
+    relay_target,
     pieces,
     mixed,
     spread,
@@ -32,6 +35,9 @@
     a_recv,
     m_send,
     m_recv,
+    b_send,
+    b_recv,
+    r_send,
     local_sem,
 ):
     tile = lax.axis_index("tile")
@@ -73,6 +79,44 @@
     for k in range(1, nm):
         member_copy(k).start()
 
+    zone_tiles = n // 4
+    zone_chips = chips // 4
+    zone = tile // zone_tiles
+    far_half = zone // 2
+    near = zone - 3 * far_half
+    depth = near * (1 - 2 * far_half)
+    inner = depth == 1
+    partner = lax.rem(tile + (1 - 2 * far_half) * zone_tiles + n, n)
+    my_chip = tile // 2
+    my_place = lax.rem(my_chip, zone_chips)
+    halves = relay_split(rows)
+    part = rows // halves
+
+    def block_copies():
+        for h in range(halves):
+            span = (slice(None), pl.ds(h * part, part), slice(None))
+            yield pltpu.make_async_remote_copy(
+                src_ref=owned_ref.at[span],
+                dst_ref=relay_block.at[span],
+                send_sem=b_send.at[h],
+                recv_sem=b_recv.at[h],
+                device_id=(partner, mem),
+                device_id_type=MESH,
+            )
+        yield pltpu.make_async_remote_copy(
+            src_ref=target_ref,
+            dst_ref=relay_target,
+            send_sem=b_send.at[halves],
+            recv_sem=b_recv.at[halves],
+            device_id=(partner, mem),
+            device_id_type=MESH,
+        )
+
+    @pl.when(inner)
+    def _():
+        for copy in reversed(list(block_copies())):
+            copy.start()
+
     def tile_copy(dest):
         return pltpu.make_async_remote_copy(
             src_ref=send_buf.at[dest],
@@ -83,6 +127,16 @@
             device_id_type=MESH,
         )
 
+    def relay_copy(h, dest):
+        return pltpu.make_async_remote_copy(
+            src_ref=relay_buf.at[dest, pl.ds(h * part, part)],
+            dst_ref=recv_ref.at[partner, pl.ds(h * part, part)],
+            send_sem=r_send.at[h, dest],
+            recv_sem=a_recv.at[partner],
+            device_id=(dest, mem),
+            device_id_type=MESH,
+        )
+
     def arrival(source):
         return pltpu.make_async_remote_copy(
             src_ref=send_buf.at[source],
@@ -93,38 +147,46 @@
             device_id_type=MESH,
         )
 
-    my_chip = tile // 2
-
-    def chip_at(p):
-        step = ((p + 1) // 2) * (1 - 2 * lax.rem(p + 1, 2))
-        return lax.rem(my_chip + step + chips, chips)
-
-    wide = jnp.concatenate([owned_ref[g] for g in range(groups)], axis=1)
+    def chip_of(their_zone, r):
+        their_zone = their_zone + far_half * (3 - 2 * their_zone)
+        return their_zone * zone_chips + lax.rem(my_place + r, zone_chips)
+
+    def direct_chip(j):
+        k = j // zone_chips
+        outer_zone = k + (k // 2) * (5 - 2 * k)
+        return chip_of(outer_zone + depth * (1 - k - outer_zone), lax.rem(j, zone_chips))
+
     row_id = lax.broadcasted_iota(jnp.int32, (groups * cols, 2 * LANES), 0)
 
-    def pack(chip):
+    def pack(wide, table_ref, chip, out_ref, span):
         first = chip * 2
-        want = jnp.concatenate([target_ref[first], target_ref[first + 1]], axis=1)
+        want = jnp.concatenate([table_ref[first], table_ref[first + 1]], axis=1)
         pick = jnp.where(row_id == want, 1.0, 0.0).astype(jnp.bfloat16)
         out = jnp.dot(wide, pick, preferred_element_type=jnp.float32).astype(jnp.bfloat16)
-        send_buf[first] = out[:, :LANES]
-        send_buf[first + 1] = out[:, LANES:]
+        out_ref[first, span] = out[:, :LANES]
+        out_ref[first + 1, span] = out[:, LANES:]
 
     def send(chip):
         for core in range(2):
-            tile_copy(chip * 2 + core).start()
-
-    pack(chip_at(1))
-
-    def step(p, carry):
-        pack(chip_at(p))
-        send(chip_at(p - 1))
+            dest = chip * 2 + core
+
+            @pl.when(dest != tile)
+            def _():
+                tile_copy(dest).start()
+
+    wide = jnp.concatenate([owned_ref[g] for g in range(groups)], axis=1)
+    whole = slice(None)
+    pack(wide, target_ref, direct_chip(0), send_buf, whole)
+
+    def step(j, carry):
+        pack(wide, target_ref, direct_chip(j), send_buf, whole)
+        send(direct_chip(j - 1))
         return carry
 
-    lax.fori_loop(2, chips, step, 0)
-    pack(my_chip)
-    send(chip_at(chips - 1))
-    other = my_chip * 2 + 1 - lax.rem(tile, 2)
+    steps = zone_chips * (4 - 2 * depth)
+    lax.fori_loop(1, steps, step, 0)
+    own_chunk = pltpu.make_async_copy(send_buf.at[tile], recv_ref.at[tile], local_sem.at[1])
+    own_chunk.start()
 
     fweight = fweight_ref[...].astype(jnp.float32)
 
@@ -138,10 +200,56 @@
         spread[pl.ds(pl.multiple_of(s * slots, slots), slots), :] = total.astype(jnp.bfloat16)
         return carry
 
-    lax.fori_loop(0, n, spread_rows, 0)
-    tile_copy(other).start()
-    own_chunk = pltpu.make_async_copy(send_buf.at[tile], recv_ref.at[tile], local_sem.at[1])
-    own_chunk.start()
+    lax.fori_loop(0, n // 2, spread_rows, 0)
+    send(direct_chip(steps - 1))
+
+    def relay_chip(j):
+        return chip_of(j // zone_chips, lax.rem(j, zone_chips))
+
+    relay_own = pltpu.make_async_copy(relay_buf.at[tile], recv_ref.at[partner], local_sem.at[4])
+
+    def relay_send(h, j):
+        for core in range(2):
+            dest = relay_chip(j) * 2 + core
+
+            @pl.when(dest != tile)
+            def _():
+                relay_copy(h, dest).start()
+
+    relay_steps = 2 * zone_chips
+
+    @pl.when(inner)
+    def _():
+        copies = list(block_copies())
+        copies[halves].wait()
+        for h in range(halves):
+            copies[h].wait()
+            span = pl.ds(h * part, part)
+            block = jnp.concatenate([relay_block[g, span] for g in range(groups)], axis=1)
+
+            def relay_step(j, carry):
+                pack(block, relay_target, relay_chip(j), relay_buf, span)
+
+                @pl.when(j > 0)
+                def _():
+                    relay_send(h, j - 1)
+
+                if h:
+
+                    @pl.when(j == 0)
+                    def _():
+                        relay_send(h - 1, relay_steps - 1)
+
+                return carry
+
+            lax.fori_loop(0, relay_steps, relay_step, 0)
+
+    lax.fori_loop(n // 2, n, spread_rows, 0)
+
+    @pl.when(inner)
+    def _():
+        relay_send(halves - 1, relay_steps - 1)
+        relay_own.start()
 
     own_piece.wait()
     spread_out = pltpu.make_async_copy(spread, spread_ref, local_sem.at[2])
@@ -163,18 +271,41 @@
 
     lax.fori_loop(0, levels, mix, 0)
 
-    def drain(k, carry):
-        source = lax.rem(tile + k, n)
-        arrival(source).wait()
-        return carry
-
-    lax.fori_loop(1, n // 2, drain, 0)
     analysis_out = pltpu.make_async_copy(mixed, analysis_ref, local_sem.at[3])
     analysis_out.start()
-    lax.fori_loop(n // 2, n, drain, 0)
+
+    def drain(k, carry):
+        other = lax.rem(tile + k, n)
+        same_half = (other // zone_tiles) // 2 == far_half
+
+        @pl.when(jnp.logical_or(jnp.logical_not(inner), same_half))
+        def _():
+            tile_copy(other).wait_send()
+
+        @pl.when(jnp.logical_and(inner, same_half))
+        def _():
+            for h in range(halves):
+                relay_copy(h, other).wait_send()
+
+        @pl.when(jnp.logical_not(jnp.logical_and(inner, other == partner)))
+        def _():
+            arrival(other).wait_recv()
+
+        return carry
+
+    lax.fori_loop(1, n, drain, 0)
+
+    @pl.when(inner)
+    def _():
+        relay_own.wait()
+
     own_chunk.wait()
     spread_out.wait()
     analysis_out.wait()
+
+
+def relay_split(rows):
+    return 2 if rows % 32 == 0 else 1
 
 
 def combine_kernel(n, groups, per_step, bias_ref, recv_ref, spread_ref, out_ref):
@@ -212,6 +343,7 @@
     obs = footprint.shape[0]
     groups = LANES // slots
     rows = channels * mem_dev // groups
+    halves = relay_split(rows)
     mem = lax.axis_index("mem")
 
     chosen = (
@@ -243,6 +375,9 @@
         out_specs=(hbm, hbm, hbm),
         scratch_shapes=[
             pltpu.VMEM((n, rows, LANES), jnp.bfloat16),
+            pltpu.VMEM((n, rows, LANES), jnp.bfloat16),
+            pltpu.VMEM((groups, rows, cols), jnp.bfloat16),
+            pltpu.VMEM((n, 1, LANES), jnp.int32),
             pltpu.VMEM((nm, levels, mem_dev, cols), jnp.bfloat16),
             pltpu.VMEM((levels, mem_dev, cols), jnp.bfloat16),
             pltpu.VMEM((n * slots, obs), jnp.bfloat16),
@@ -250,7 +385,10 @@
             pltpu.SemaphoreType.DMA((n,)),
             pltpu.SemaphoreType.DMA((nm,)),
             pltpu.SemaphoreType.DMA((nm,)),
-            pltpu.SemaphoreType.DMA((4,)),
+            pltpu.SemaphoreType.DMA((halves + 1,)),
+            pltpu.SemaphoreType.DMA((halves + 1,)),
+            pltpu.SemaphoreType.DMA((halves, n)),
+            pltpu.SemaphoreType.DMA((5,)),
         ],
         compiler_params=pltpu.CompilerParams(
             collective_id=0, has_side_effects=True, vmem_limit_bytes=48 * 1024 * 1024

time: 112 us -> 91.3 us (0.82)
  Pallas kernels: 100 us -> 79.7 us
    pallas_call x1, Pallas kernels: 93.3 us -> 72.7 us  [shards(): pl.pallas_call(functools.partial(exchange_kernel, n, nm), out_shape=(jax....]
where the time goes in v2:
time: 91.3 us; the launch traced here: 91 us
  Pallas kernels  79.7 us (87%)
  local copies, waits for them, and re-layouts  6.5 us (7%)
  matrix products  3.21 us (4%)
    pallas_call x1, Pallas kernels, shards(): pl.pallas_call(functools.partial(exchange_kernel, n, nm), out_shape=(jax....  72.7 us
    pallas_call x1, Pallas kernels, shards(): pl.pallas_call(functools.partial(combine_kernel, n, groups, per_step), ou...  6.96 us
    unnamed x13, local copies, waits for them, and re-layouts  4.14 us
    dot_general x1, matrix products, shards(): jnp.einsum('cl,klx->ckx', selected, background, preferred_element_type=jn...  3.21 us

profile of v2, /device:TPU:1, one launch (start us, length us, event | category | flops | bytes accessed | tf_op | source)
XLA Modules:
  0.0 91.0 jit_solution(2321258112496682755)
XLA Ops:
  0.6 0.0 copy-start
  0.7 0.1 add.31
  0.7 0.1 add.32
  0.8 0.8 maximum_bitcast_fusion
  1.7 0.8 constant_dynamic-slice_fusion
  2.5 0.1 copy.17
  2.6 0.1 add.30
  2.7 0.8 copy.18.mean_ref
  3.5 0.0 copy-done
  3.5 3.2 %fusion.4 = bf16[96,40,128]{2,0,1:T(8,128)(2,1)S(1)} fusion(bf16[40,137,128]{2,0,1:T(8,128)(2,1)} %param.13, bf16[8461,137]{0,1:T(8,128)(2,1)S(1)} %copy-done, s32[96]{0:T(128)} %param.15), kind=kOutput, calls=%fused_computation.5 | convolution fusion | flops 358551552 | bytes 4704618 | tf_op jit(solution)/shard_map/cl,klx->ckx/dot_general | solution.py:355
  6.7 0.0 copy-start.2
  6.7 0.0 copy-start.3
  6.8 0.0 copy-start.4
  6.8 0.0 copy-start.5
  6.8 0.4 copy.15
  7.2 0.9 %copy-done.2 = bf16[40,137,128]{2,0,1:T(8,128)(2,1)S(1)} copy-done((bf16[40,137,128]{2,0,1:T(8,128)(2,1)S(1)}, bf16[40,137,128]{2,0,1:T(8,128)(2,1)}, u32[]{:S(2)}) %copy-start.2) | copy-done | bytes 1402904
  8.1 0.0 copy-done.3
  8.1 0.0 copy-done.4
  8.1 72.7 %exchange.1 = (bf16[16,960,128]{2,1,0:T(8,128)(2,1)}, bf16[137,40,128]{2,1,0:T(8,128)(2,1)S(1)}, bf16[512,512]{1,0:T(8,128)(2,1)S(1)}) custom-call(bf16[4,960,128]{2,1,0:T(8,128)(2,1)S(1)} %bitcast.16, s32[16,1,128]{2,1,0:T(1,128)S(1)} %broadcast_add_fusion.target_ref, bf16[137,40,128]{2,1,0:T(8,128)(2,1)S(1)} %bitcast.17, bf16[2,40,40]{2,1,0:T(8,128)(2,1)S(1)} %bitcast.19, ...), custom_call_target="tpu_custom_call" | custom-call | tf_op jit(solution)/shard_map/exchange/pallas_call | solution.py:367
  80.8 0.0 copy-done.5
  80.8 0.0 copy-start.1
  80.8 2.1 %copy-done.1 = bf16[16,960,128]{2,1,0:T(8,128)(2,1)S(1)} copy-done((bf16[16,960,128]{2,1,0:T(8,128)(2,1)S(1)}, bf16[16,960,128]{2,1,0:T(8,128)(2,1)}, u32[]{:S(2)}) %copy-start.1) | copy-done | bytes 3932184
  83.0 7.0 %combine.1 = f32[4,24,40,512]{3,2,1,0:T(8,128)} custom-call(f32[96]{0:T(128)S(1)} %copy-done.5, bf16[16,960,128]{2,1,0:T(8,128)(2,1)S(1)} %copy-done.1, bf16[512,512]{1,0:T(8,128)(2,1)S(1)} %get-tuple-element.7.spread_ref), custom_call_target="tpu_custom_call" | custom-call | tf_op jit(solution)/shard_map/combine/pallas_call | solution.py:410
  89.9 1.1 %copy.26 = bf16[40,137,128]{2,0,1:T(8,128)(2,1)} copy(bf16[40,137,128]{2,0,1:T(8,128)(2,1)S(1)} %bitcast.18) | data formatting | bytes 2805760
  (3 shorter events, 0.0 us)
Async XLA Ops:
  0.6 2.9 %copy-start = (bf16[8461,137]{0,1:T(8,128)(2,1)S(1)}, bf16[8461,137]{0,1:T(8,128)(2,1)}, u32[]{:S(2)}) copy-start(bf16[8461,137]{0,1:T(8,128)(2,1)} %param.14) | copy-start | bytes 6954946
  6.7 1.4 %copy-start.2 = (bf16[40,137,128]{2,0,1:T(8,128)(2,1)S(1)}, bf16[40,137,128]{2,0,1:T(8,128)(2,1)}, u32[]{:S(2)}) copy-start(bf16[40,137,128]{2,0,1:T(8,128)(2,1)} %param.10) | copy-start | bytes 4208644
  6.7 1.3 %copy-start.3 = (s32[512,4]{0,1:T(4,128)S(1)}, s32[512,4]{0,1:T(4,128)}, u32[]{:S(2)}) copy-start(s32[512,4]{0,1:T(4,128)} %param.17) | copy-start | bytes 24580
  6.8 1.3 %copy-start.4 = (bf16[512,4]{0,1:T(4,128)(2,1)S(1)}, bf16[512,4]{0,1:T(4,128)(2,1)}, u32[]{:S(2)}) copy-start(bf16[512,4]{0,1:T(4,128)(2,1)} %param.18) | copy-start | bytes 12292
  6.8 74.1 %copy-start.5 = (f32[96]{0:T(128)S(1)}, f32[96]{0:T(128)}, u32[]{:S(2)}) copy-start(f32[96]{0:T(128)} %bias_ref.1) | copy-start | bytes 1156
  80.8 2.1 %copy-start.1 = (bf16[16,960,128]{2,1,0:T(8,128)(2,1)S(1)}, bf16[16,960,128]{2,1,0:T(8,128)(2,1)}, u32[]{:S(2)}) copy-start(bf16[16,960,128]{2,1,0:T(8,128)(2,1)} %get-tuple-element.6.recv_ref) | copy-start | bytes 11796484

commit v3 on v2

--- a/solution.py
+++ b/solution.py
@@ -31,6 +31,7 @@
     pieces,
     mixed,
     spread,
+    mean_wide,
     a_send,
     a_recv,
     m_send,
@@ -257,9 +258,11 @@
     for k in range(1, nm):
         member_copy(k).wait()
 
+    mean_wide[...] = mean_ref[...].astype(jnp.float32)
+
     def mix(l, carry):
         total = jnp.broadcast_to(
-            mean_ref[l].astype(jnp.float32), (weight_ref.shape[1], cols)
+            mean_wide[pl.ds(l, 1), :], (weight_ref.shape[1], cols)
         )
         mixture = jnp.zeros_like(total)
         for p in range(nm):
@@ -313,14 +316,21 @@
     slots = spread_ref.shape[0] // n
     per_group = out_ref.shape[1] * pl.num_programs(0)
     members = out_ref.shape[2]
+    rows = recv_ref.shape[1]
     blocks = [recv_ref[s] for s in range(n)]
+    stacked = jnp.concatenate(
+        [
+            jnp.concatenate([block[:, g * slots : (g + 1) * slots] for block in blocks], axis=1)
+            for g in range(groups)
+        ],
+        axis=0,
+    )
+    prior = jnp.dot(stacked, spread_ref[...], preferred_element_type=jnp.float32)
     for g in range(groups):
-        lanes = slice(g * slots, (g + 1) * slots)
-        stacked = jnp.concatenate([block[:, lanes] for block in blocks], axis=1)
-        prior = jnp.dot(stacked, spread_ref[...], preferred_element_type=jnp.float32)
         for c in range(per_step):
+            first = g * rows + c * members
             bias = bias_ref[g * per_group + step * per_step + c]
-            out_ref[g, c] = prior[c * members : (c + 1) * members, :] + bias
+            out_ref[g, c] = prior[first : first + members, :] + bias
 
 
 def shards(
@@ -381,6 +391,7 @@
             pltpu.VMEM((nm, levels, mem_dev, cols), jnp.bfloat16),
             pltpu.VMEM((levels, mem_dev, cols), jnp.bfloat16),
             pltpu.VMEM((n * slots, obs), jnp.bfloat16),
+            pltpu.VMEM((levels, cols), jnp.float32),
             pltpu.SemaphoreType.DMA((n,)),
             pltpu.SemaphoreType.DMA((n,)),
             pltpu.SemaphoreType.DMA((nm,)),
@@ -391,7 +402,7 @@
             pltpu.SemaphoreType.DMA((5,)),
         ],
         compiler_params=pltpu.CompilerParams(
-            collective_id=0, has_side_effects=True, vmem_limit_bytes=48 * 1024 * 1024
+            collective_id=0, has_side_effects=True, vmem_limit_bytes=24 * 1024 * 1024
         ),
         name="exchange",
     )(
@@ -399,7 +410,7 @@
         target,
         jnp.transpose(anomalies, (1, 0, 2)),
         weights,
-        background_mean[:, None, :],
+        background_mean,
         jnp.transpose(footprint),
         jnp.transpose(footprint_weight),
     )
@@ -417,7 +428,7 @@
             pl.BlockSpec((n * slots, obs), lambda i: (0, 0)),
         ],
         out_specs=pl.BlockSpec((groups, per_step, mem_dev, obs), lambda i: (0, i, 0, 0)),
-        compiler_params=pltpu.CompilerParams(vmem_limit_bytes=48 * 1024 * 1024),
+        compiler_params=pltpu.CompilerParams(vmem_limit_bytes=24 * 1024 * 1024),
         name="combine",
     )(channel_bias, received, spread)
     return analysis_members, prior.reshape(channels, mem_dev, obs)

time: 91.3 us -> 88.1 us (0.965)
  local copies, waits for them, and re-layouts: 6.5 us -> 3.56 us
    unnamed x13, local copies, waits for them, and re-layouts: 4.14 us -> 2.03 us
where the time goes in v3:
time: 88.1 us; the launch traced here: 87.9 us
  Pallas kernels  79.6 us (90%)
  local copies, waits for them, and re-layouts  3.56 us (4%)
  matrix products  3.21 us (4%)
    pallas_call x1, Pallas kernels, shards(): pl.pallas_call(functools.partial(exchange_kernel, n, nm), out_shape=(jax....  72.7 us
    pallas_call x1, Pallas kernels, shards(): pl.pallas_call(functools.partial(combine_kernel, n, groups, per_step), ou...  6.82 us
    dot_general x1, matrix products, shards(): jnp.einsum('cl,klx->ckx', selected, background, preferred_element_type=jn...  3.21 us
    unnamed x13, local copies, waits for them, and re-layouts  2.03 us

profile of v3, /device:TPU:1, one launch (start us, length us, event | category | flops | bytes accessed | tf_op | source)
XLA Modules:
  0.0 87.9 jit_solution(4108473689298697173)
XLA Ops:
  0.6 0.0 copy-start
  0.7 0.1 add.31
  0.7 0.1 add.32
  0.8 0.8 maximum_bitcast_fusion
  1.7 0.8 constant_dynamic-slice_fusion
  2.5 0.1 copy.17
  2.6 0.1 add.30
  2.7 0.0 copy-done
  2.7 3.2 %fusion.4 = bf16[96,40,128]{2,0,1:T(8,128)(2,1)S(1)} fusion(bf16[40,137,128]{2,0,1:T(8,128)(2,1)} %param.13, bf16[8461,137]{0,1:T(8,128)(2,1)S(1)} %copy-done, s32[96]{0:T(128)} %param.15), kind=kOutput, calls=%fused_computation.5 | convolution fusion | flops 358551552 | bytes 4704618 | tf_op jit(solution)/shard_map/cl,klx->ckx/dot_general | solution.py:365
  5.9 0.0 copy-start.1
  5.9 0.0 copy-start.2
  5.9 0.0 copy-start.3
  5.9 0.0 copy-start.4
  5.9 0.0 copy-start.5
  6.0 0.4 copy.15
  6.3 0.9 %copy-done.1 = bf16[40,137,128]{2,0,1:T(8,128)(2,1)S(1)} copy-done((bf16[40,137,128]{2,0,1:T(8,128)(2,1)S(1)}, bf16[40,137,128]{2,0,1:T(8,128)(2,1)}, u32[]{:S(2)}) %copy-start.1) | copy-done | bytes 1402904
  7.2 0.0 copy-done.2
  7.3 0.0 copy-done.3
  7.3 0.0 copy-done.4
  7.3 72.7 %exchange.1 = (bf16[16,960,128]{2,1,0:T(8,128)(2,1)S(1)}, bf16[137,40,128]{2,1,0:T(8,128)(2,1)S(1)}, bf16[512,512]{1,0:T(8,128)(2,1)S(1)}) custom-call(bf16[4,960,128]{2,1,0:T(8,128)(2,1)S(1)} %bitcast.15, s32[16,1,128]{2,1,0:T(1,128)S(1)} %broadcast_add_fusion.target_ref, bf16[137,40,128]{2,1,0:T(8,128)(2,1)S(1)} %bitcast.16, ...), custom_call_target="tpu_custom_call" | custom-call | tf_op jit(solution)/shard_map/exchange/pallas_call | solution.py:377
  80.0 0.0 copy-done.5
  80.0 6.8 %combine.1 = f32[4,24,40,512]{3,2,1,0:T(8,128)} custom-call(f32[96]{0:T(128)S(1)} %copy-done.5, bf16[16,960,128]{2,1,0:T(8,128)(2,1)S(1)} %get-tuple-element.6.recv_ref, bf16[512,512]{1,0:T(8,128)(2,1)S(1)} %get-tuple-element.7.spread_ref), custom_call_target="tpu_custom_call" | custom-call | tf_op jit(solution)/shard_map/combine/pallas_call | solution.py:421
  86.8 1.1 %copy.25 = bf16[40,137,128]{2,0,1:T(8,128)(2,1)} copy(bf16[40,137,128]{2,0,1:T(8,128)(2,1)S(1)} %bitcast.17) | data formatting | bytes 2805760
  (3 shorter events, 0.0 us)
Async XLA Ops:
  0.6 2.0 %copy-start = (bf16[8461,137]{0,1:T(8,128)(2,1)S(1)}, bf16[8461,137]{0,1:T(8,128)(2,1)}, u32[]{:S(2)}) copy-start(bf16[8461,137]{0,1:T(8,128)(2,1)} %param.14) | copy-start | bytes 6954946
  5.9 1.4 %copy-start.1 = (bf16[40,137,128]{2,0,1:T(8,128)(2,1)S(1)}, bf16[40,137,128]{2,0,1:T(8,128)(2,1)}, u32[]{:S(2)}) copy-start(bf16[40,137,128]{2,0,1:T(8,128)(2,1)} %param.10) | copy-start | bytes 4208644
  5.9 1.3 %copy-start.2 = (bf16[137,128]{1,0:T(8,128)(2,1)S(1)}, bf16[137,128]{1,0:T(8,128)(2,1)}, u32[]{:S(2)}) copy-start(bf16[137,128]{1,0:T(8,128)(2,1)} %mean_ref.1) | copy-start | bytes 105220
  5.9 1.3 %copy-start.3 = (s32[512,4]{0,1:T(4,128)S(1)}, s32[512,4]{0,1:T(4,128)}, u32[]{:S(2)}) copy-start(s32[512,4]{0,1:T(4,128)} %param.17) | copy-start | bytes 24580
  5.9 1.3 %copy-start.4 = (bf16[512,4]{0,1:T(4,128)(2,1)S(1)}, bf16[512,4]{0,1:T(4,128)(2,1)}, u32[]{:S(2)}) copy-start(bf16[512,4]{0,1:T(4,128)(2,1)} %param.18) | copy-start | bytes 12292
  5.9 74.1 %copy-start.5 = (f32[96]{0:T(128)S(1)}, f32[96]{0:T(128)}, u32[]{:S(2)}) copy-start(f32[96]{0:T(128)} %bias_ref.1) | copy-start | bytes 1156
